TPU v7x, 32 devices: a whole 2x2x4 slice. The times are simulated.
32 devices in a mesh: groups: 2 (over y), seq: 4 (over z), batch: 2 (over x), head: 2 (over core).
Axes of the slice: x: 2, y: 2, z: 4, core: 2. Of those that a mesh axis runs over, the one named last changes fastest.
Arguments:
- hidden_in: bfloat16 [64, 4096], P(('groups', 'batch'), 'seq'), parts along dimension 0, may hold values from -400 to 400
- norm_gain_vector: bfloat16 [4096], P('seq'), may hold values from 0.099609375 to 1.8984375
- w_query: bfloat16 [4096, 4096], P('seq', 'head'), may hold values from -0.09375 to 0.09375
- key_cache_rows: bfloat16 [64, 4096, 128], P(('groups', 'batch'), 'seq'), parts along dimension 0, may hold values from -360 to 360
- value_cache_rows: bfloat16 [64, 4096, 128], P(('groups', 'batch'), 'seq'), parts along dimension 0, may hold values from -6 to 6
- k_new: bfloat16 [64, 128], P(('groups', 'batch')), parts along dimension 0, may hold values from -360 to 360
- v_new: bfloat16 [64, 128], P(('groups', 'batch')), parts along dimension 0, may hold values from -6 to 6
- lengths: int32 [64], P(('groups', 'batch')), parts along dimension 0, may hold values from 1 to 4096, as said below
- w_out: bfloat16 [4096, 4096], P('head', 'seq'), may hold values from -0.09375 to 0.09375
Outputs:
- layer_out: float32 [64, 4096], P(('groups', 'batch'), ('seq', 'head')), parts along dimension 0
There are 2 independent parts, one for each index of `groups`. A program takes and returns all parts, laid end to end along the dimension named above; an argument that names none is the same for every part. Nothing has to cross between parts.
Inputs may be any that keep to these rules, and one draw needn't show every extreme that they name: `lengths`: every sequence has at least one cached position; some sequence of each draw uses all 4096.
All inputs are finite; a program needn't handle non-finite values.
Results may differ from a plain program's by a relative error of at most 0.008.
Values sent between devices are 32-bit elements; how exact they have to be, the bound alone decides.
A program may use at most 64 MiB of HBM per device.

v0:
```python
import functools

import jax
import jax.numpy as jnp
from jax import lax
from jax.experimental import pallas as pl
from jax.experimental.pallas import tpu as pltpu
from jax.sharding import PartitionSpec as P

HD = 128
EPS = 1e-05
MESH = pl.DeviceIdType.MESH
F32 = jnp.float32
BF16 = jnp.bfloat16


def chunk_edges(heads, cuts):
    step = heads // cuts
    return [(c * step, (c + 1) * step) for c in range(cuts)]


def kernel(
    n,
    heads,
    rows,
    cuts,
    m,
    subs,
    lens_ref,
    hidden_hbm,
    gain_hbm,
    wq_hbm,
    keys_hbm,
    values_hbm,
    knew_hbm,
    vnew_hbm,
    wout_hbm,
    out_ref,
    hid,
    gain,
    wq,
    kbuf,
    vbuf,
    knew,
    vnew,
    wout,
    newf,
    qsend,
    qrecv,
    qturn,
    qall,
    asend,
    arecv,
    att,
    hsend,
    hrecv,
    small_sem,
    wq_sem,
    k_sem,
    v_sem,
    wo_sem,
    qs_send,
    qs_recv,
    qg_send,
    qg_recv,
    as_send,
    as_recv,
    ag_send,
    ag_recv,
    h_send,
    h_recv,
):
    me = lax.axis_index("seq")
    core = lax.axis_index("head")
    other = 1 - core
    first = (n - m) // 2
    share = rows // m
    piece = share // subs
    block = keys_hbm.shape[1]
    width = wq_hbm.shape[0] * n
    edges = chunk_edges(heads, cuts)
    owning = jnp.logical_and(me >= first, me < first + m)
    my_slot = jnp.clip(me - first, 0, m - 1)
    slots = [lax.rem(my_slot + k, m) for k in range(m)]
    away = [(n // 2 + k) % n for k in range(n)]
    away = [k for k in away if k]

    barrier = pltpu.get_barrier_semaphore()

    def greet(s):
        pl.semaphore_signal(
            barrier, inc=1, device_id={"seq": s, "head": core}, device_id_type=MESH
        )

    for s in range(n):
        meet = me != s
        if not first <= s < first + m:
            meet = jnp.logical_and(meet, owning)
        pl.when(meet)(functools.partial(greet, s))
    pl.semaphore_signal(barrier, inc=1, device_id={"head": other}, device_id_type=MESH)

    small = [
        pltpu.make_async_copy(src, dst, small_sem.at[i])
        for i, (src, dst) in enumerate(
            ((hidden_hbm, hid), (gain_hbm, gain), (knew_hbm, knew), (vnew_hbm, vnew))
        )
    ]
    for copy in small:
        copy.start()
    wq_copies = []
    for c, (lo, hi) in enumerate(edges):
        cols = pl.ds(lo * HD, (hi - lo) * HD)
        wq_copies.append(pltpu.make_async_copy(wq_hbm.at[:, cols], wq.at[:, cols], wq_sem.at[c]))
        wq_copies[-1].start()
    k_copies, v_copies = [], []
    for k in range(m):
        group = pl.ds(slots[k] * share, share)
        k_copies.append(pltpu.make_async_copy(keys_hbm.at[group], kbuf.at[k], k_sem.at[k]))
        v_copies.append(pltpu.make_async_copy(values_hbm.at[group], vbuf.at[k], v_sem.at[k]))
        k_copies[-1].start()
        v_copies[-1].start()
    half = wout_hbm.shape[1] // 2
    wo_copies = []
    for i, side in enumerate((other, core)):
        cols = pl.ds(pl.multiple_of(side * half, HD), half)
        wo_copies.append(pltpu.make_async_copy(wout_hbm.at[:, cols], wout.at[i], wo_sem.at[i]))
        wo_copies[-1].start()

    small[0].wait()
    small[1].wait()
    x = hid[...].astype(F32)
    squares = jnp.sum(x * x, axis=-1, keepdims=True)
    scaled = x * gain[...].astype(F32)
    upper = scaled.astype(BF16)
    lower = (scaled - upper.astype(F32)).astype(BF16)
    both = jnp.concatenate([upper, lower], axis=0)
    for p in range(m):
        qsend[p, 0] = jnp.broadcast_to(squares[p * share : (p + 1) * share], (share, HD))
    qs = [[None] * m for _ in edges]

    def arrivals(c, s):
        lo, hi = edges[c]
        span = pl.ds(0 if c == 0 else lo + 1, hi + 1 - (0 if c == 0 else lo + 1))
        return pltpu.make_async_remote_copy(
            src_ref=qsend.at[0, span],
            dst_ref=qrecv.at[s, span],
            send_sem=qs_send.at[c, 0],
            recv_sem=qs_recv.at[c, s],
            device_id={"seq": me, "head": core},
            device_id_type=MESH,
        )

    for c, (lo, hi) in enumerate(edges):
        wq_copies[c].wait()
        product = jnp.dot(both, wq[:, lo * HD : hi * HD], preferred_element_type=F32)
        part = product[:rows] + product[rows:]
        for h in range(lo, hi):
            for p in range(m):
                qsend[p, h + 1] = part[
                    p * share : (p + 1) * share, (h - lo) * HD : (h - lo + 1) * HD
                ]
        if c == 0:
            pl.semaphore_wait(barrier, jnp.where(owning, n, m + 1))
        start = 0 if c == 0 else lo + 1
        span = pl.ds(start, hi + 1 - start)
        for k in reversed(range(m)):
            qs[c][k] = pltpu.make_async_remote_copy(
                src_ref=qsend.at[slots[k], span],
                dst_ref=qrecv.at[me, span],
                send_sem=qs_send.at[c, k],
                recv_sem=qs_recv.at[c, me],
                device_id={"seq": slots[k] + first, "head": core},
                device_id_type=MESH,
            )
            if k:
                qs[c][k].start()
            else:
                pl.when(jnp.logical_not(owning))(qs[c][k].start)

    small[2].wait()
    small[3].wait()
    newf[0] = knew[...].astype(F32)
    newf[1] = vnew[...].astype(F32)

    def gathers(u):
        return [
            pltpu.make_async_remote_copy(
                src_ref=qall.at[my_slot, pl.ds(u * piece, piece)],
                dst_ref=qall.at[my_slot, pl.ds(u * piece, piece)],
                send_sem=qg_send.at[u, i],
                recv_sem=qg_recv.at[u, my_slot],
                device_id={"seq": lax.rem(me + k, n), "head": core},
                device_id_type=MESH,
            )
            for i, k in enumerate(away)
        ]

    @pl.when(owning)
    def _():
        for c in range(len(edges)):
            for s in range(1, n):
                arrivals(c, lax.rem(me + s, n)).wait_recv()
        total = qsend[my_slot]
        for s in range(1, n):
            total = total + qrecv[lax.rem(me + s, n)]
        inv = lax.rsqrt(total[0] / width + EPS) * (1.0 / HD**0.5)
        qturn[...] = (total[1:] * inv[None]).astype(BF16).astype(F32)
        for u in range(subs):
            for r in range(u * piece, (u + 1) * piece):
                qall[my_slot, r] = qturn[:, r, :]
            for copy in gathers(u):
                copy.start()

    lanes = lax.broadcasted_iota(jnp.int32, (heads, HD), 1)
    positions = me * block + lax.broadcasted_iota(jnp.int32, (heads, block), 1)
    sends = []
    for k in range(m):
        for u in range(subs):
            i = k * subs + u
            arrival = pltpu.make_async_remote_copy(
                src_ref=qall.at[my_slot, pl.ds(u * piece, piece)],
                dst_ref=qall.at[slots[k], pl.ds(u * piece, piece)],
                send_sem=qg_send.at[u, 0],
                recv_sem=qg_recv.at[u, slots[k]],
                device_id={"seq": me, "head": core},
                device_id_type=MESH,
            )
            if k:
                arrival.wait_recv()
            else:
                pl.when(jnp.logical_not(owning))(arrival.wait_recv)
            if u == 0:
                k_copies[k].wait()
            scores, own = [], []
            for r in range(piece):
                q = qall[slots[k], u * piece + r]
                scores.append(
                    lax.dot_general(
                        q.astype(BF16),
                        kbuf[k, u * piece + r],
                        (((1,), (1,)), ((), ())),
                        preferred_element_type=F32,
                    )
                )
                row = slots[k] * share + u * piece + r
                own.append(jnp.sum(q * newf[0, pl.ds(row, 1)], axis=-1, keepdims=True))
            if u == 0:
                v_copies[k].wait()
            stats = jnp.zeros((heads, HD), F32)
            for r in range(piece):
                live = positions < lens_ref[slots[k] * share + u * piece + r]
                masked = jnp.where(live, scores[r], -jnp.inf)
                top = jnp.maximum(jnp.max(masked, axis=-1, keepdims=True), own[r])
                weights = jnp.exp(masked - top)
                weight = jnp.sum(weights, axis=-1, keepdims=True)
                stats = jnp.where(lanes == 2 * r, top, stats)
                stats = jnp.where(lanes == 2 * r + 1, weight, stats)
                asend[i, r] = jnp.dot(
                    weights.astype(BF16), vbuf[k, u * piece + r], preferred_element_type=F32
                )
            asend[i, piece] = stats
            sends.append(
                pltpu.make_async_remote_copy(
                    src_ref=asend.at[i],
                    dst_ref=arecv.at[me, u],
                    send_sem=as_send.at[i],
                    recv_sem=as_recv.at[u, me],
                    device_id={"seq": slots[k] + first, "head": core},
                    device_id_type=MESH,
                )
            )
            if k:
                sends[-1].start()
            else:
                pl.when(jnp.logical_not(owning))(sends[-1].start)

    def returns(u):
        return [
            pltpu.make_async_remote_copy(
                src_ref=att.at[pl.ds(my_slot * share + u * piece, piece)],
                dst_ref=att.at[pl.ds(my_slot * share + u * piece, piece)],
                send_sem=ag_send.at[u, i],
                recv_sem=ag_recv.at[u, my_slot],
                device_id={"seq": lax.rem(me + k, n), "head": core},
                device_id_type=MESH,
            )
            for i, k in enumerate(away)
        ]

    @pl.when(owning)
    def _():
        for u in range(subs):
            others = [lax.rem(me + s, n) for s in range(1, n)]
            for s in others:
                pltpu.make_async_remote_copy(
                    src_ref=asend.at[0],
                    dst_ref=arecv.at[s, u],
                    send_sem=as_send.at[0],
                    recv_sem=as_recv.at[u, s],
                    device_id={"seq": me, "head": core},
                    device_id_type=MESH,
                ).wait_recv()
            stats = [asend[u, piece]] + [arecv[s, u, piece] for s in others]
            for r in range(piece):
                row = my_slot * share + u * piece + r
                tops = [s[:, 2 * r : 2 * r + 1] for s in stats]
                own = jnp.sum(
                    qall[my_slot, u * piece + r] * newf[0, pl.ds(row, 1)], axis=-1, keepdims=True
                )
                top = functools.reduce(jnp.maximum, tops)
                fresh = jnp.exp(own - top)
                totals = fresh
                summed = fresh * newf[1, pl.ds(row, 1)]
                for s in range(n):
                    factor = jnp.exp(tops[s] - top)
                    totals = totals + stats[s][:, 2 * r + 1 : 2 * r + 2] * factor
                    summed = summed + (arecv[others[s - 1], u, r] if s else asend[u, r]) * factor
                att[row] = (summed / totals).astype(BF16).astype(F32)
            for copy in returns(u):
                copy.start()

    for copy in wo_copies:
        copy.wait()
    for j in range(m):
        for u in range(subs):
            group = pl.ds(j * share + u * piece, piece)
            arrival = pltpu.make_async_remote_copy(
                src_ref=att.at[group],
                dst_ref=att.at[group],
                send_sem=ag_send.at[u, 0],
                recv_sem=ag_recv.at[u, j],
                device_id={"seq": me, "head": core},
                device_id_type=MESH,
            )
            pl.when(me != first + j)(arrival.wait_recv)

    attended = jnp.concatenate([att[:, h, :] for h in range(heads)], axis=1).astype(BF16)
    hsend[...] = jnp.dot(attended, wout[0], preferred_element_type=F32)
    swap = pltpu.make_async_remote_copy(
        src_ref=hsend,
        dst_ref=hrecv,
        send_sem=h_send,
        recv_sem=h_recv,
        device_id={"head": other},
        device_id_type=MESH,
    )
    swap.start()
    kept = jnp.dot(attended, wout[1], preferred_element_type=F32)
    swap.wait_recv()
    out_ref[...] = kept + hrecv[...]

    for c in range(len(edges)):
        for k in range(1, m):
            qs[c][k].wait_send()
    for copy in sends[subs:]:
        copy.wait_send()
    swap.wait_send()

    @pl.when(owning)
    def _():
        for u in range(subs):
            for copy in gathers(u) + returns(u):
                copy.wait_send()

    @pl.when(jnp.logical_not(owning))
    def _():
        for c in range(len(edges)):
            qs[c][0].wait_send()
        for copy in sends[:subs]:
            copy.wait_send()


def solution(mesh):
    n = mesh.shape["seq"]
    cuts = 2
    m = max(n // 2, 1)
    subs = 2

    def shards(hidden, gain, wq, keys, values, knew, vnew, lengths, wout):
        rows, depth = hidden.shape
        heads = wq.shape[1] // HD
        share = rows // m
        piece = share // subs
        block = keys.shape[1]
        half = wout.shape[1] // 2
        anywhere = pl.BlockSpec(memory_space=pl.ANY)
        dma = pltpu.SemaphoreType.DMA
        return pl.pallas_call(
            functools.partial(kernel, n, heads, rows, cuts, m, subs),
            out_shape=jax.ShapeDtypeStruct((rows, half), F32),
            in_specs=[pl.BlockSpec(memory_space=pltpu.SMEM)] + [anywhere] * 8,
            out_specs=pl.BlockSpec(memory_space=pltpu.VMEM),
            scratch_shapes=[
                pltpu.VMEM((rows, depth), BF16),
                pltpu.VMEM((1, depth), BF16),
                pltpu.VMEM(wq.shape, BF16),
                pltpu.VMEM((m, share, block, HD), BF16),
                pltpu.VMEM((m, share, block, HD), BF16),
                pltpu.VMEM((rows, HD), BF16),
                pltpu.VMEM((rows, HD), BF16),
                pltpu.VMEM((2, wout.shape[0], half), BF16),
                pltpu.VMEM((2, rows, HD), F32),
                pltpu.VMEM((m, heads + 1, share, HD), F32),
                pltpu.VMEM((n, heads + 1, share, HD), F32),
                pltpu.VMEM((heads, share, HD), F32),
                pltpu.VMEM((m, share, heads, HD), F32),
                pltpu.VMEM((m * subs, piece + 1, heads, HD), F32),
                pltpu.VMEM((n, subs, piece + 1, heads, HD), F32),
                pltpu.VMEM((rows, heads, HD), F32),
                pltpu.VMEM((rows, half), F32),
                pltpu.VMEM((rows, half), F32),
                dma((4,)),
                dma((cuts,)),
                dma((m,)),
                dma((m,)),
                dma((2,)),
                dma((cuts, m)),
                dma((cuts, n)),
                dma((subs, n)),
                dma((subs, m)),
                dma((m * subs,)),
                dma((subs, n)),
                dma((subs, n)),
                dma((subs, m)),
                dma(()),
                dma(()),
            ],
            compiler_params=pltpu.CompilerParams(collective_id=0, has_side_effects=True),
            name="decode_step",
        )(lengths, hidden, gain.reshape(1, -1), wq, keys, values, knew, vnew, wout)

    placed = (
        P(("groups", "batch"), "seq"),
        P("seq"),
        P("seq", "head"),
        P(("groups", "batch"), "seq", None),
        P(("groups", "batch"), "seq", None),
        P(("groups", "batch"), None),
        P(("groups", "batch"), None),
        P(("groups", "batch")),
        P("head", "seq"),
    )
    return jax.shard_map(
        shards,
        mesh=mesh,
        in_specs=placed,
        out_specs=P(("groups", "batch"), ("seq", "head")),
        check_vma=False,
    )
```

profile of v0, /device:TPU:0, one launch (start us, length us, event | category | flops | bytes accessed | tf_op | source)
XLA Modules:
  0.0 29.8 jit_solution(8356044066967496546)
XLA Ops:
  0.0 1.3 %reshape.3.gain_hbm = bf16[1,1024]{1,0:T(2,128)(2,1)} reshape(bf16[1024]{0:T(1024)(128)(2,1)} %param.10) | data formatting | bytes 4096 | tf_op jit(solution)/shard_map/reshape | solution.py:430
  1.3 27.1 %decode_step.1 = f32[16,512]{1,0:T(8,128)} custom-call(s32[16]{0:T(128)} %lens_ref.1, bf16[16,1024]{1,0:T(8,128)(2,1)} %hidden_hbm.1, bf16[1,1024]{1,0:T(2,128)(2,1)} %reshape.3.gain_hbm, bf16[1024,2048]{1,0:T(8,128)(2,1)} %wq_hbm.1, bf16[16,1024,128]{2,1,0:T(8,128)(2,1)} %keys_hbm.1, bf16[16,1024,128]{2,1,0:T(8,128)(2,1)} %values_hbm.1, ...), custom_call_target="tpu_custom_call" | custom-call | tf_op jit(solution)/shard_map/decode_step/pallas_call | solution.py:388
  28.4 1.4 %copy.11 = f32[16,512]{1,0:T(8,128)} copy(f32[16,512]{1,0:T(8,128)} %decode_step.1) | data formatting | bytes 65536
where the time goes:
time: 30.2 us; the launch traced here: 29.8 us
  Pallas kernels  27.1 us (90%)
  local copies, waits for them, and re-layouts  2.65 us (9%)
    pallas_call x1, Pallas kernels, shards(): pl.pallas_call(functools.partial(kernel, n, heads, rows, cuts, m, subs),...  27.1 us
    unnamed x1, local copies, waits for them, and re-layouts  1.38 us
    reshape x1, local copies, waits for them, and re-layouts, shards(): gain.reshape(1, -1)  1.28 us

commit v1 on v0

--- a/solution.py
+++ b/solution.py
@@ -26,7 +26,7 @@
     cuts,
     m,
     subs,
-    lens_ref,
+    lens_hbm,
     hidden_hbm,
     gain_hbm,
     wq_hbm,
@@ -36,6 +36,7 @@
     vnew_hbm,
     wout_hbm,
     out_ref,
+    lens_ref,
     hid,
     gain,
     wq,
@@ -102,35 +103,43 @@
     small = [
         pltpu.make_async_copy(src, dst, small_sem.at[i])
         for i, (src, dst) in enumerate(
-            ((hidden_hbm, hid), (gain_hbm, gain), (knew_hbm, knew), (vnew_hbm, vnew))
+            (
+                (hidden_hbm, hid),
+                (gain_hbm, gain),
+                (knew_hbm, knew),
+                (vnew_hbm, vnew),
+                (lens_hbm, lens_ref),
+            )
         )
     ]
-    for copy in small:
+    for copy in small[:2]:
         copy.start()
     wq_copies = []
     for c, (lo, hi) in enumerate(edges):
         cols = pl.ds(lo * HD, (hi - lo) * HD)
         wq_copies.append(pltpu.make_async_copy(wq_hbm.at[:, cols], wq.at[:, cols], wq_sem.at[c]))
         wq_copies[-1].start()
+    for copy in small[2:]:
+        copy.start()
     k_copies, v_copies = [], []
     for k in range(m):
         group = pl.ds(slots[k] * share, share)
         k_copies.append(pltpu.make_async_copy(keys_hbm.at[group], kbuf.at[k], k_sem.at[k]))
         v_copies.append(pltpu.make_async_copy(values_hbm.at[group], vbuf.at[k], v_sem.at[k]))
-        k_copies[-1].start()
-        v_copies[-1].start()
     half = wout_hbm.shape[1] // 2
     wo_copies = []
     for i, side in enumerate((other, core)):
         cols = pl.ds(pl.multiple_of(side * half, HD), half)
         wo_copies.append(pltpu.make_async_copy(wout_hbm.at[:, cols], wout.at[i], wo_sem.at[i]))
-        wo_copies[-1].start()
 
     small[0].wait()
     small[1].wait()
     x = hid[...].astype(F32)
     squares = jnp.sum(x * x, axis=-1, keepdims=True)
-    scaled = x * gain[...].astype(F32)
+    g = gain[...].astype(F32)
+    scaled = jnp.concatenate(
+        [x[:, i * HD : (i + 1) * HD] * g[i : i + 1] for i in range(g.shape[0])], axis=1
+    )
     upper = scaled.astype(BF16)
     lower = (scaled - upper.astype(F32)).astype(BF16)
     both = jnp.concatenate([upper, lower], axis=0)
@@ -152,6 +161,9 @@
 
     for c, (lo, hi) in enumerate(edges):
         wq_copies[c].wait()
+        if c == cuts - 1:
+            for copy in [x for pair in zip(k_copies, v_copies) for x in pair] + wo_copies:
+                copy.start()
         product = jnp.dot(both, wq[:, lo * HD : hi * HD], preferred_element_type=F32)
         part = product[:rows] + product[rows:]
         for h in range(lo, hi):
@@ -177,8 +189,8 @@
             else:
                 pl.when(jnp.logical_not(owning))(qs[c][k].start)
 
-    small[2].wait()
-    small[3].wait()
+    for copy in small[2:]:
+        copy.wait()
     newf[0] = knew[...].astype(F32)
     newf[1] = vnew[...].astype(F32)
 
@@ -387,12 +399,13 @@
         dma = pltpu.SemaphoreType.DMA
         return pl.pallas_call(
             functools.partial(kernel, n, heads, rows, cuts, m, subs),
-            out_shape=jax.ShapeDtypeStruct((rows, half), F32),
-            in_specs=[pl.BlockSpec(memory_space=pltpu.SMEM)] + [anywhere] * 8,
+            out_shape=pltpu.VMEM((rows, half), F32),
+            in_specs=[anywhere] * 9,
             out_specs=pl.BlockSpec(memory_space=pltpu.VMEM),
             scratch_shapes=[
+                pltpu.SMEM((rows,), jnp.int32),
                 pltpu.VMEM((rows, depth), BF16),
-                pltpu.VMEM((1, depth), BF16),
+                pltpu.VMEM((depth // HD, HD), BF16),
                 pltpu.VMEM(wq.shape, BF16),
                 pltpu.VMEM((m, share, block, HD), BF16),
                 pltpu.VMEM((m, share, block, HD), BF16),
@@ -409,7 +422,7 @@
                 pltpu.VMEM((rows, heads, HD), F32),
                 pltpu.VMEM((rows, half), F32),
                 pltpu.VMEM((rows, half), F32),
-                dma((4,)),
+                dma((5,)),
                 dma((cuts,)),
                 dma((m,)),
                 dma((m,)),
@@ -427,7 +440,7 @@
             ],
             compiler_params=pltpu.CompilerParams(collective_id=0, has_side_effects=True),
             name="decode_step",
-        )(lengths, hidden, gain.reshape(1, -1), wq, keys, values, knew, vnew, wout)
+        )(lengths, hidden, gain.reshape(-1, HD), wq, keys, values, knew, vnew, wout)
 
     placed = (
         P(("groups", "batch"), "seq"),

time: 30.2 us -> 25.7 us (0.85)
  Pallas kernels: 27.1 us -> 24.6 us
  local copies, waits for them, and re-layouts: 2.65 us -> 0.62 us
    pallas_call x1, Pallas kernels: 27.1 us -> 24.6 us  [shards(): pl.pallas_call(functools.partial(kernel, n, heads, rows, cuts, m, subs),...]
    reshape x1 -> x0, local copies, waits for them, and re-layouts: 1.28 us -> none  [shards(): gain.reshape(1, -1)]
    unnamed x1, local copies, waits for them, and re-layouts: 1.38 us -> 0.62 us
where the time goes in v1:
time: 25.7 us; the launch traced here: 25.3 us
  Pallas kernels  24.6 us (96%)
  local copies, waits for them, and re-layouts  0.62 us (2%)
    pallas_call x1, Pallas kernels, shards(): pl.pallas_call(functools.partial(kernel, n, heads, rows, cuts, m, subs),...  24.6 us
    unnamed x1, local copies, waits for them, and re-layouts  0.62 us

profile of v1, /device:TPU:0, one launch (start us, length us, event | category | flops | bytes accessed | tf_op | source)
XLA Modules:
  0.0 25.3 jit_solution(15732864083119493362)
XLA Ops:
  0.0 24.6 %decode_step.1 = f32[16,512]{1,0:T(8,128)S(1)} custom-call(s32[16]{0:T(128)} %lens_hbm.1, bf16[16,1024]{1,0:T(8,128)(2,1)} %hidden_hbm.1, bf16[8,128]{1,0:T(8,128)(2,1)} %bitcast.1, bf16[1024,2048]{1,0:T(8,128)(2,1)} %wq_hbm.1, bf16[16,1024,128]{2,1,0:T(8,128)(2,1)} %keys_hbm.1, bf16[16,1024,128]{2,1,0:T(8,128)(2,1)} %values_hbm.1, ...), custom_call_target="tpu_custom_call" | custom-call | tf_op jit(solution)/shard_map/decode_step/pallas_call | solution.py:400
  24.7 0.6 %copy.11 = f32[16,512]{1,0:T(8,128)} copy(f32[16,512]{1,0:T(8,128)S(1)} %decode_step.1) | data formatting | bytes 65536

commit v2 on v1

v2 whole, which is shorter than its diff:
```python
import functools

import jax
import jax.numpy as jnp
from jax import lax
from jax.experimental import pallas as pl
from jax.experimental.pallas import tpu as pltpu
from jax.sharding import PartitionSpec as P

HD = 128
EPS = 1e-05
MESH = pl.DeviceIdType.MESH
F32 = jnp.float32
BF16 = jnp.bfloat16
CUTS = 4
CHUNKS = 2
FARFIRST = 0


def outside_in(n):
    order = []
    for k in range((n + 1) // 2):
        order += [k] if k == n - 1 - k else [k, n - 1 - k]
    return order


def kernel(
    n,
    heads,
    rows,
    m,
    cuts,
    chunks,
    lens_hbm,
    hidden_hbm,
    gain_hbm,
    wq_hbm,
    keys_hbm,
    values_hbm,
    knew_hbm,
    vnew_hbm,
    wout_hbm,
    out_ref,
    lens_ref,
    hid,
    gain,
    wq,
    kbuf,
    vbuf,
    newb,
    wout,
    newf,
    qsend,
    qrecv,
    qturn,
    qown,
    qall,
    asend,
    arecv,
    aout,
    att,
    hsend,
    hrecv,
    tally,
    in_sem,
    wq_sem,
    kv_sem,
    wo_sem,
    qs_send,
    qs_recv,
    qg_send,
    qg_recv,
    as_send,
    as_recv,
    ag_send,
    ag_recv,
    h_sem,
):
    me = lax.axis_index("seq")
    core = lax.axis_index("head")
    other = 1 - core
    first = (n - m) // 2
    share = rows // m
    piece = share // 2
    half_rows = rows // 2
    block = keys_hbm.shape[1]
    width = wq_hbm.shape[0] * n
    step = heads // cuts
    hc = heads // chunks
    full = 2 * hc
    per_chunk = cuts // chunks
    on_chip = jnp.logical_and(me >= first, me < first + m)
    owning = jnp.logical_and(on_chip, core == 1)
    resting = jnp.logical_not(owning)
    my_j = jnp.clip(me - first, 0, m - 1)
    order = outside_in(n)

    def device(z, h):
        return {"seq": z, "head": h}

    def is_me(z, h):
        return jnp.logical_and(me == z, core == h)

    def not_me(z, h):
        return jnp.logical_not(is_me(z, h))

    barrier = pltpu.get_barrier_semaphore()

    def greet(z, h):
        pl.semaphore_signal(barrier, inc=1, device_id=device(z, h), device_id_type=MESH)

    for z in order:
        for h in (0, 1):
            meet = not_me(z, h)
            if h == 0 or not first <= z < first + m:
                partner = jnp.logical_and(me == z, core == 1 - h)
                meet = jnp.logical_and(meet, jnp.logical_or(owning, partner))
            pl.when(meet)(functools.partial(greet, z, h))
    greeted = jnp.where(owning, 2 * n - 1, jnp.where(on_chip, m, m + 1))

    ins = [
        pltpu.make_async_copy(src, dst, in_sem.at[i])
        for i, src, dst in (
            (0, hidden_hbm, hid),
            (1, gain_hbm, gain),
            (2, knew_hbm, newb.at[0]),
            (2, vnew_hbm, newb.at[1]),
            (3, lens_hbm, lens_ref),
        )
    ]
    for copy in ins[:2]:
        copy.start()
    wq_copies = []
    for c in range(cuts):
        cols = pl.ds(c * step * HD, step * HD)
        wq_copies.append(pltpu.make_async_copy(wq_hbm.at[:, cols], wq.at[:, cols], wq_sem.at[c]))
        wq_copies[-1].start()
    for copy in ins[2:]:
        copy.start()
    group = pl.ds(core * half_rows, half_rows)
    half = wout_hbm.shape[1] // 2
    later = [
        pltpu.make_async_copy(keys_hbm.at[group], kbuf, kv_sem.at[0]),
        pltpu.make_async_copy(values_hbm.at[group], vbuf, kv_sem.at[1]),
    ]
    for i, side in enumerate((other, core)):
        cols = pl.ds(pl.multiple_of(side * half, HD), half)
        later.append(pltpu.make_async_copy(wout_hbm.at[:, cols], wout.at[i], wo_sem))

    ins[0].wait()
    ins[1].wait()
    x = hid[...].astype(F32)
    x = jnp.concatenate(
        [
            x[u * half_rows + j * piece : u * half_rows + (j + 1) * piece]
            for j in range(m)
            for u in (0, 1)
        ],
        axis=0,
    )
    squares = jnp.sum(x * x, axis=-1, keepdims=True)
    g = gain[...].astype(F32)
    scaled = jnp.concatenate(
        [x[:, i * HD : (i + 1) * HD] * g[i : i + 1] for i in range(g.shape[0])], axis=1
    )
    upper = scaled.astype(BF16)
    lower = (scaled - upper.astype(F32)).astype(BF16)
    both = jnp.concatenate([upper, lower], axis=0)
    for j in range(m):
        qsend[j, 0] = jnp.broadcast_to(squares[j * share : (j + 1) * share], (share, HD))

    def span(c):
        return pl.ds(0 if c == 0 else c * step + 1, step + (1 if c == 0 else 0))

    def partial_send(c, j):
        return pltpu.make_async_remote_copy(
            src_ref=qsend.at[j, span(c)],
            dst_ref=qrecv.at[2 * me + core, span(c)],
            send_sem=qs_send,
            recv_sem=qs_recv.at[c // per_chunk],
            device_id=device(first + j, 1),
            device_id_type=MESH,
        )

    def place_own(j, c):
        qrecv[2 * me + 1, span(c)] = qsend[j, span(c)]

    for c in range(cuts):
        wq_copies[c].wait()
        if c == cuts - 1:
            for copy in later:
                copy.start()
        product = jnp.dot(
            both, wq[:, c * step * HD : (c + 1) * step * HD], preferred_element_type=F32
        )
        part = product[:rows] + product[rows:]
        for h in range(step):
            for j in range(m):
                qsend[j, c * step + h + 1] = part[
                    j * share : (j + 1) * share, h * HD : (h + 1) * HD
                ]
        if c == 0:
            pl.semaphore_wait(barrier, greeted)
        for j in range(m):
            pl.when(not_me(first + j, 1))(partial_send(c, j).start)
            pl.when(is_me(first + j, 1))(functools.partial(place_own, j, c))

    pltpu.make_async_copy(newb, newb, in_sem.at[2]).wait()
    ins[4].wait()
    newf[...] = newb[...].astype(F32)

    def query_sends(c):
        return [
            (
                not_me(z, u),
                pltpu.make_async_remote_copy(
                    src_ref=qall.at[c, my_j] if u else qown.at[c],
                    dst_ref=qall.at[c, my_j],
                    send_sem=qg_send,
                    recv_sem=qg_recv.at[c, my_j],
                    device_id=device(z, u),
                    device_id_type=MESH,
                ),
            )
            for u in (0, 1)
            for z in order
        ]

    @pl.when(owning)
    def _():
        for c in range(chunks):
            lo = 0 if c == 0 else 1 + c * hc
            arrived = qrecv.at[pl.ds(0, 2 * n - 1), pl.ds(lo, 1 + (c + 1) * hc - lo)]
            pltpu.make_async_copy(arrived, arrived, qs_recv.at[c]).wait()
            total = functools.reduce(jnp.add, [qrecv[2 * z + 1, 0] for z in range(n)])
            inv = lax.rsqrt(total / width + EPS) * (1.0 / HD**0.5)
            for h in (0, 1):
                planes = pl.ds(1 + c * hc, hc)
                q = functools.reduce(jnp.add, [qrecv[2 * z + h, planes] for z in range(n)])
                qturn[h * hc : (h + 1) * hc] = (q * inv[None]).astype(BF16).astype(F32)
            for r in range(piece):
                qown[c, r] = qturn[:, r, :]
                qall[c, my_j, r] = qturn[:, piece + r, :]
            for go, copy in query_sends(c):
                pl.when(go)(copy.start)

    lanes = lax.broadcasted_iota(jnp.int32, (full, HD), 1)
    lanes = lanes - lax.broadcasted_iota(jnp.int32, (full, HD), 0) // 8 * (2 * piece)
    positions = me * block + lax.broadcasted_iota(jnp.int32, (full, block), 1)

    def keep_own(c):
        arecv[c, 1, me] = asend[c, my_j]

    def result_send(c, j):
        return pltpu.make_async_remote_copy(
            src_ref=asend.at[c, j],
            dst_ref=arecv.at[c, core, me],
            send_sem=as_send,
            recv_sem=as_recv.at[c, core],
            device_id=device(first + j, 1),
            device_id_type=MESH,
        )

    for c in range(chunks):
        for k in range(m):
            far = c == chunks - 1 and FARFIRST
            j = lax.rem(my_j + (m - 1 - k if far else k), m)
            arrival = pltpu.make_async_remote_copy(
                src_ref=qall.at[c, j],
                dst_ref=qall.at[c, j],
                send_sem=qg_send,
                recv_sem=qg_recv.at[c, j],
                device_id=device(me, other),
                device_id_type=MESH,
            )
            pl.when(not_me(first + j, 1))(arrival.wait_recv)
            if c == 0 and k == 0:
                later[0].wait()
            scores, own = [], []
            for r in range(piece):
                q = qall[c, j, r]
                scores.append(
                    lax.dot_general(
                        q.astype(BF16),
                        kbuf[j * piece + r],
                        (((1,), (1,)), ((), ())),
                        preferred_element_type=F32,
                    )
                )
                row = core * half_rows + j * piece + r
                own.append(jnp.sum(q * newf[0, pl.ds(row, 1)], axis=-1, keepdims=True))
            if c == 0 and k == 0:
                later[1].wait()
            stats = jnp.zeros((full, HD), F32)
            for r in range(piece):
                live = positions < lens_ref[core * half_rows + j * piece + r]
                masked = jnp.where(live, scores[r], -jnp.inf)
                top = jnp.maximum(jnp.max(masked, axis=-1, keepdims=True), own[r])
                weights = jnp.exp(masked - top)
                weight = jnp.sum(weights, axis=-1, keepdims=True)
                stats = jnp.where(lanes == 2 * r, top, stats)
                stats = jnp.where(lanes == 2 * r + 1, weight, stats)
                asend[c, j, r * full : (r + 1) * full] = jnp.dot(
                    weights.astype(BF16), vbuf[j * piece + r], preferred_element_type=F32
                )
            asend[c, j, piece * full : piece * full + 8] = functools.reduce(
                jnp.add, [stats[i : i + 8] for i in range(0, full, 8)]
            )
            pl.when(not_me(first + j, 1))(result_send(c, j).start)
            pl.when(is_me(first + j, 1))(functools.partial(keep_own, c))

    def returns(c, u):
        group = pl.ds(u * half_rows + my_j * piece, piece)
        return [
            (
                not_me(z, h),
                pltpu.make_async_remote_copy(
                    src_ref=att.at[c, group] if h else aout.at[c, u],
                    dst_ref=att.at[c, group],
                    send_sem=ag_send,
                    recv_sem=ag_recv.at[c],
                    device_id=device(z, h),
                    device_id_type=MESH,
                ),
            )
            for z in order
            for h in (0, 1)
        ]

    @pl.when(owning)
    def _():
        for c in range(chunks):
            for u in (1, 0):
                arrived = arecv.at[c, u, pl.ds(0, n - u)]
                pltpu.make_async_copy(arrived, arrived, as_recv.at[c, u]).wait()
                stats = [arecv[c, u, z, piece * full : piece * full + 8] for z in range(n)]
                for r in range(piece):
                    row = u * half_rows + my_j * piece + r

                    def column(s, i):
                        at = [2 * piece * t + 2 * r + i for t in range(full // 8)]
                        return jnp.concatenate([s[:, a : a + 1] for a in at], axis=0)

                    tops = [column(s, 0) for s in stats]
                    q = qall[c, my_j, r] if u else qown[c, r]
                    own = jnp.sum(q * newf[0, pl.ds(row, 1)], axis=-1, keepdims=True)
                    top = functools.reduce(jnp.maximum, tops)
                    fresh = jnp.exp(own - top)
                    totals = fresh
                    summed = fresh * newf[1, pl.ds(row, 1)]
                    for z in range(n):
                        factor = jnp.exp(tops[z] - top)
                        totals = totals + column(stats[z], 1) * factor
                        summed = summed + arecv[c, u, z, r * full : (r + 1) * full] * factor
                    result = (summed / totals).astype(BF16).astype(F32)
                    aout[c, u, r] = result[:hc]
                    att[c, row] = result[hc:]
                for go, copy in returns(c, u):
                    pl.when(go)(copy.start)

    sent, kept = None, None
    for c in range(chunks):
        for owner, count in ((owning, rows - share), (resting, rows)):
            arrived = att.at[c, pl.ds(0, count)]
            pl.when(owner)(pltpu.make_async_copy(arrived, arrived, ag_recv.at[c]).wait)
        if c == 0:
            pltpu.make_async_copy(wout, wout, wo_sem).wait()
        attended = jnp.concatenate([att[c, :, h, :] for h in range(hc)], axis=1).astype(BF16)
        deep = slice(c * hc * HD, (c + 1) * hc * HD)
        product = jnp.dot(attended, wout[0, deep], preferred_element_type=F32)
        sent = product if sent is None else sent + product
        if c == chunks - 1:
            hsend[...] = sent
            swap = pltpu.make_async_remote_copy(
                src_ref=hsend,
                dst_ref=hrecv,
                send_sem=h_sem.at[0],
                recv_sem=h_sem.at[1],
                device_id=device(me, other),
                device_id_type=MESH,
            )
            swap.start()
        product = jnp.dot(attended, wout[1, deep], preferred_element_type=F32)
        kept = product if kept is None else kept + product
    swap.wait_recv()
    out_ref[...] = kept + hrecv[...]
    swap.wait_send()

    def drain(ref, sem):
        pltpu.make_async_copy(ref, ref, sem).wait()

    @pl.when(resting)
    def _():
        drain(qsend, qs_send)
        drain(asend, as_send)

    @pl.when(owning)
    def _():
        drain(qsend.at[pl.ds(0, m - 1)], qs_send)
        drain(asend.at[:, pl.ds(0, m - 1)], as_send)
        drain(tally, qg_send)
        drain(tally, ag_send)


def solution(mesh):
    n = mesh.shape["seq"]
    m = max(n // 2, 2)

    def shards(hidden, gain, wq, keys, values, knew, vnew, lengths, wout):
        rows, depth = hidden.shape
        heads = wq.shape[1] // HD
        share = rows // m
        piece = share // 2
        block = keys.shape[1]
        half = wout.shape[1] // 2
        hc = heads // CHUNKS
        anywhere = pl.BlockSpec(memory_space=pl.ANY)
        dma = pltpu.SemaphoreType.DMA
        return pl.pallas_call(
            functools.partial(kernel, n, heads, rows, m, CUTS, CHUNKS),
            out_shape=pltpu.VMEM((rows, half), F32),
            in_specs=[anywhere] * 9,
            out_specs=pl.BlockSpec(memory_space=pltpu.VMEM),
            scratch_shapes=[
                pltpu.SMEM((rows,), jnp.int32),
                pltpu.VMEM((rows, depth), BF16),
                pltpu.VMEM((depth // HD, HD), BF16),
                pltpu.VMEM(wq.shape, BF16),
                pltpu.VMEM((rows // 2, block, HD), BF16),
                pltpu.VMEM((rows // 2, block, HD), BF16),
                pltpu.VMEM((2, rows, HD), BF16),
                pltpu.VMEM((2, wout.shape[0], half), BF16),
                pltpu.VMEM((2, rows, HD), F32),
                pltpu.VMEM((m, heads + 1, share, HD), F32),
                pltpu.VMEM((2 * n, heads + 1, share, HD), F32),
                pltpu.VMEM((2 * hc, share, HD), F32),
                pltpu.VMEM((CHUNKS, piece, 2 * hc, HD), F32),
                pltpu.VMEM((CHUNKS, m, piece, 2 * hc, HD), F32),
                pltpu.VMEM((CHUNKS, m, piece * 2 * hc + 8, HD), F32),
                pltpu.VMEM((CHUNKS, 2, n, piece * 2 * hc + 8, HD), F32),
                pltpu.VMEM((CHUNKS, 2, piece, hc, HD), F32),
                pltpu.VMEM((CHUNKS, rows, hc, HD), F32),
                pltpu.VMEM((rows, half), F32),
                pltpu.VMEM((rows, half), F32),
                pltpu.VMEM((CHUNKS, 2 * n - 1, piece, 2 * hc, HD), F32),
                dma((4,)),
                dma((CUTS,)),
                dma((2,)),
                dma(()),
                dma(()),
                dma((CHUNKS,)),
                dma(()),
                dma((CHUNKS, m)),
                dma(()),
                dma((CHUNKS, 2)),
                dma(()),
                dma((CHUNKS,)),
                dma((2,)),
            ],
            compiler_params=pltpu.CompilerParams(collective_id=0, has_side_effects=True),
            name="decode_step",
        )(lengths, hidden, gain.reshape(-1, HD), wq, keys, values, knew, vnew, wout)

    placed = (
        P(("groups", "batch"), "seq"),
        P("seq"),
        P("seq", "head"),
        P(("groups", "batch"), "seq", None),
        P(("groups", "batch"), "seq", None),
        P(("groups", "batch"), None),
        P(("groups", "batch"), None),
        P(("groups", "batch")),
        P("head", "seq"),
    )
    return jax.shard_map(
        shards,
        mesh=mesh,
        in_specs=placed,
        out_specs=P(("groups", "batch"), ("seq", "head")),
        check_vma=False,
    )
```

time: 25.7 us -> 23.5 us (0.914); the launches traced: 25.3 us -> 23.4 us
  Pallas kernels: 24.6 us -> 22.8 us
    pallas_call x1, Pallas kernels: 24.6 us -> 22.8 us  [shards(): pl.pallas_call(functools.partial(kernel, n, heads, rows, m, CUTS, CHUNKS)...]
where the time goes in v2:
time: 23.5 us; the launch traced here: 23.4 us
  Pallas kernels  22.8 us (97%)
  local copies, waits for them, and re-layouts  0.62 us (3%)
    pallas_call x1, Pallas kernels, shards(): pl.pallas_call(functools.partial(kernel, n, heads, rows, m, CUTS, CHUNKS)...  22.8 us
    unnamed x1, local copies, waits for them, and re-layouts  0.62 us

profile of v2, /device:TPU:0, one launch (start us, length us, event | category | flops | bytes accessed | tf_op | source)
XLA Modules:
  0.0 23.4 jit_solution(6430400248914825750)
XLA Ops:
  0.0 22.8 %decode_step.1 = f32[16,512]{1,0:T(8,128)S(1)} custom-call(s32[16]{0:T(128)} %lens_hbm.1, bf16[16,1024]{1,0:T(8,128)(2,1)} %hidden_hbm.1, bf16[8,128]{1,0:T(8,128)(2,1)} %bitcast.1, bf16[1024,2048]{1,0:T(8,128)(2,1)} %wq_hbm.1, bf16[16,1024,128]{2,1,0:T(8,128)(2,1)} %keys_hbm.1, bf16[16,1024,128]{2,1,0:T(8,128)(2,1)} %values_hbm.1, ...), custom_call_target="tpu_custom_call" | custom-call | tf_op jit(solution)/shard_map/decode_step/pallas_call | solution.py:419
  22.8 0.6 %copy.11 = f32[16,512]{1,0:T(8,128)} copy(f32[16,512]{1,0:T(8,128)S(1)} %decode_step.1) | data formatting | bytes 65536

commit v3 on v2

--- a/solution.py
+++ b/solution.py
@@ -12,9 +12,8 @@
 MESH = pl.DeviceIdType.MESH
 F32 = jnp.float32
 BF16 = jnp.bfloat16
-CUTS = 4
+EDGES = (0, 2, 4, 8, 16)
 CHUNKS = 2
-FARFIRST = 0
 
 
 def outside_in(n):
@@ -85,10 +84,9 @@
     half_rows = rows // 2
     block = keys_hbm.shape[1]
     width = wq_hbm.shape[0] * n
-    step = heads // cuts
     hc = heads // chunks
     full = 2 * hc
-    per_chunk = cuts // chunks
+    wide = full // 8 * piece
     on_chip = jnp.logical_and(me >= first, me < first + m)
     owning = jnp.logical_and(on_chip, core == 1)
     resting = jnp.logical_not(owning)
@@ -131,8 +129,8 @@
     for copy in ins[:2]:
         copy.start()
     wq_copies = []
-    for c in range(cuts):
-        cols = pl.ds(c * step * HD, step * HD)
+    for c in range(len(cuts) - 1):
+        cols = pl.ds(cuts[c] * HD, (cuts[c + 1] - cuts[c]) * HD)
         wq_copies.append(pltpu.make_async_copy(wq_hbm.at[:, cols], wq.at[:, cols], wq_sem.at[c]))
         wq_copies[-1].start()
     for copy in ins[2:]:
@@ -170,14 +168,15 @@
         qsend[j, 0] = jnp.broadcast_to(squares[j * share : (j + 1) * share], (share, HD))
 
     def span(c):
-        return pl.ds(0 if c == 0 else c * step + 1, step + (1 if c == 0 else 0))
+        start = cuts[c] + 1 if c else 0
+        return pl.ds(start, cuts[c + 1] + 1 - start)
 
     def partial_send(c, j):
         return pltpu.make_async_remote_copy(
             src_ref=qsend.at[j, span(c)],
             dst_ref=qrecv.at[2 * me + core, span(c)],
             send_sem=qs_send,
-            recv_sem=qs_recv.at[c // per_chunk],
+            recv_sem=qs_recv.at[cuts[c] // hc],
             device_id=device(first + j, 1),
             device_id_type=MESH,
         )
@@ -185,18 +184,18 @@
     def place_own(j, c):
         qrecv[2 * me + 1, span(c)] = qsend[j, span(c)]
 
-    for c in range(cuts):
+    for c in range(len(cuts) - 1):
         wq_copies[c].wait()
-        if c == cuts - 1:
+        if c == len(cuts) - 2:
             for copy in later:
                 copy.start()
         product = jnp.dot(
-            both, wq[:, c * step * HD : (c + 1) * step * HD], preferred_element_type=F32
+            both, wq[:, cuts[c] * HD : cuts[c + 1] * HD], preferred_element_type=F32
         )
         part = product[:rows] + product[rows:]
-        for h in range(step):
+        for h in range(cuts[c + 1] - cuts[c]):
             for j in range(m):
-                qsend[j, c * step + h + 1] = part[
+                qsend[j, cuts[c] + h + 1] = part[
                     j * share : (j + 1) * share, h * HD : (h + 1) * HD
                 ]
         if c == 0:
@@ -222,8 +221,8 @@
                     device_id_type=MESH,
                 ),
             )
+            for z in reversed(order)
             for u in (0, 1)
-            for z in order
         ]
 
     @pl.when(owning)
@@ -245,7 +244,7 @@
                 pl.when(go)(copy.start)
 
     lanes = lax.broadcasted_iota(jnp.int32, (full, HD), 1)
-    lanes = lanes - lax.broadcasted_iota(jnp.int32, (full, HD), 0) // 8 * (2 * piece)
+    lanes = lanes - lax.broadcasted_iota(jnp.int32, (full, HD), 0) // 8 * piece
     positions = me * block + lax.broadcasted_iota(jnp.int32, (full, block), 1)
 
     def keep_own(c):
@@ -263,8 +262,7 @@
 
     for c in range(chunks):
         for k in range(m):
-            far = c == chunks - 1 and FARFIRST
-            j = lax.rem(my_j + (m - 1 - k if far else k), m)
+            j = lax.rem(my_j + k, m)
             arrival = pltpu.make_async_remote_copy(
                 src_ref=qall.at[c, j],
                 dst_ref=qall.at[c, j],
@@ -298,8 +296,8 @@
                 top = jnp.maximum(jnp.max(masked, axis=-1, keepdims=True), own[r])
                 weights = jnp.exp(masked - top)
                 weight = jnp.sum(weights, axis=-1, keepdims=True)
-                stats = jnp.where(lanes == 2 * r, top, stats)
-                stats = jnp.where(lanes == 2 * r + 1, weight, stats)
+                for i, column in enumerate((top, weight, own[r])):
+                    stats = jnp.where(lanes == i * wide + r, column, stats)
                 asend[c, j, r * full : (r + 1) * full] = jnp.dot(
                     weights.astype(BF16), vbuf[j * piece + r], preferred_element_type=F32
                 )
@@ -309,7 +307,7 @@
             pl.when(not_me(first + j, 1))(result_send(c, j).start)
             pl.when(is_me(first + j, 1))(functools.partial(keep_own, c))
 
-    def returns(c, u):
+    def returns(c, u, stops):
         group = pl.ds(u * half_rows + my_j * piece, piece)
         return [
             (
@@ -323,7 +321,7 @@
                     device_id_type=MESH,
                 ),
             )
-            for z in order
+            for z in stops
             for h in (0, 1)
         ]
 
@@ -334,28 +332,36 @@
                 arrived = arecv.at[c, u, pl.ds(0, n - u)]
                 pltpu.make_async_copy(arrived, arrived, as_recv.at[c, u]).wait()
                 stats = [arecv[c, u, z, piece * full : piece * full + 8] for z in range(n)]
+                tops = [s[:, :wide] for s in stats]
+                top = functools.reduce(jnp.maximum, tops)
+                fresh = jnp.exp(stats[0][:, 2 * wide : 3 * wide] - top)
+                factors = [jnp.exp(t - top) for t in tops]
+                totals = fresh
+                for z in range(n):
+                    totals = totals + stats[z][:, wide : 2 * wide] * factors[z]
+                inverse = 1.0 / totals
+                fresh = fresh * inverse
+                factors = [f * inverse for f in factors]
                 for r in range(piece):
                     row = u * half_rows + my_j * piece + r
-
-                    def column(s, i):
-                        at = [2 * piece * t + 2 * r + i for t in range(full // 8)]
-                        return jnp.concatenate([s[:, a : a + 1] for a in at], axis=0)
-
-                    tops = [column(s, 0) for s in stats]
-                    q = qall[c, my_j, r] if u else qown[c, r]
-                    own = jnp.sum(q * newf[0, pl.ds(row, 1)], axis=-1, keepdims=True)
-                    top = functools.reduce(jnp.maximum, tops)
-                    fresh = jnp.exp(own - top)
-                    totals = fresh
-                    summed = fresh * newf[1, pl.ds(row, 1)]
-                    for z in range(n):
-                        factor = jnp.exp(tops[z] - top)
-                        totals = totals + column(stats[z], 1) * factor
-                        summed = summed + arecv[c, u, z, r * full : (r + 1) * full] * factor
-                    result = (summed / totals).astype(BF16).astype(F32)
-                    aout[c, u, r] = result[:hc]
-                    att[c, row] = result[hc:]
-                for go, copy in returns(c, u):
+                    for t in range(full // 8):
+                        at = t * piece + r
+                        result = fresh[:, at : at + 1] * newf[1, pl.ds(row, 1)]
+                        for z in range(n):
+                            part = arecv[c, u, z, r * full + t * 8 : r * full + t * 8 + 8]
+                            result = result + part * factors[z][:, at : at + 1]
+                        result = result.astype(BF16).astype(F32)
+                        if t * 8 < hc:
+                            aout[c, u, r, t * 8 : t * 8 + 8] = result
+                        else:
+                            att[c, row, t * 8 - hc : t * 8 - hc + 8] = result
+                if c < chunks - 1:
+                    ready = returns(c, u, order)
+                else:
+                    ready = returns(c, u, order[:2])
+                    if u == 0:
+                        ready += returns(c, 1, order[2:]) + returns(c, 0, order[2:])
+                for go, copy in ready:
                     pl.when(go)(copy.start)
 
     sent, kept = None, None
@@ -414,10 +420,11 @@
         block = keys.shape[1]
         half = wout.shape[1] // 2
         hc = heads // CHUNKS
+        cuts = tuple(heads * e // EDGES[-1] for e in EDGES)
         anywhere = pl.BlockSpec(memory_space=pl.ANY)
         dma = pltpu.SemaphoreType.DMA
         return pl.pallas_call(
-            functools.partial(kernel, n, heads, rows, m, CUTS, CHUNKS),
+            functools.partial(kernel, n, heads, rows, m, cuts, CHUNKS),
             out_shape=pltpu.VMEM((rows, half), F32),
             in_specs=[anywhere] * 9,
             out_specs=pl.BlockSpec(memory_space=pltpu.VMEM),
@@ -444,7 +451,7 @@
                 pltpu.VMEM((rows, half), F32),
                 pltpu.VMEM((CHUNKS, 2 * n - 1, piece, 2 * hc, HD), F32),
                 dma((4,)),
-                dma((CUTS,)),
+                dma((len(cuts) - 1,)),
                 dma((2,)),
                 dma(()),
                 dma(()),

time: 23.5 us -> 22.4 us (0.953)
  Pallas kernels: 22.8 us -> 21.7 us
    pallas_call x1, Pallas kernels: 22.8 us -> 21.7 us  [shards(): pl.pallas_call(functools.partial(kernel, n, heads, rows, m, cuts, CHUNKS)...]
where the time goes in v3:
time: 22.4 us; the launch traced here: 22.3 us
  Pallas kernels  21.7 us (97%)
  local copies, waits for them, and re-layouts  0.62 us (3%)
    pallas_call x1, Pallas kernels, shards(): pl.pallas_call(functools.partial(kernel, n, heads, rows, m, cuts, CHUNKS)...  21.7 us
    unnamed x1, local copies, waits for them, and re-layouts  0.62 us

profile of v3, /device:TPU:0, one launch (start us, length us, event | category | flops | bytes accessed | tf_op | source)
XLA Modules:
  0.0 22.3 jit_solution(46118208101175111)
XLA Ops:
  0.0 21.7 %decode_step.1 = f32[16,512]{1,0:T(8,128)S(1)} custom-call(s32[16]{0:T(128)} %lens_hbm.1, bf16[16,1024]{1,0:T(8,128)(2,1)} %hidden_hbm.1, bf16[8,128]{1,0:T(8,128)(2,1)} %bitcast.1, bf16[1024,2048]{1,0:T(8,128)(2,1)} %wq_hbm.1, bf16[16,1024,128]{2,1,0:T(8,128)(2,1)} %keys_hbm.1, bf16[16,1024,128]{2,1,0:T(8,128)(2,1)} %values_hbm.1, ...), custom_call_target="tpu_custom_call" | custom-call | tf_op jit(solution)/shard_map/decode_step/pallas_call | solution.py:426
  21.7 0.6 %copy.11 = f32[16,512]{1,0:T(8,128)} copy(f32[16,512]{1,0:T(8,128)S(1)} %decode_step.1) | data formatting | bytes 65536

commit v4 on v3

--- a/solution.py
+++ b/solution.py
@@ -14,6 +14,7 @@
 BF16 = jnp.bfloat16
 EDGES = (0, 2, 4, 8, 16)
 CHUNKS = 2
+UNITS = (0, 4, 8, 16)
 
 
 def outside_in(n):
@@ -30,6 +31,7 @@
     m,
     cuts,
     chunks,
+    units,
     lens_hbm,
     hidden_hbm,
     gain_hbm,
@@ -54,6 +56,10 @@
     qturn,
     qown,
     qall,
+    kturn,
+    ssend,
+    srecv,
+    coef,
     asend,
     arecv,
     aout,
@@ -69,6 +75,8 @@
     qs_recv,
     qg_send,
     qg_recv,
+    ss_send,
+    ss_recv,
     as_send,
     as_recv,
     ag_send,
@@ -86,7 +94,10 @@
     width = wq_hbm.shape[0] * n
     hc = heads // chunks
     full = 2 * hc
-    wide = full // 8 * piece
+    subs = 1
+    part_rows = piece
+    squared = units[1]
+    each = 2 * part_rows
     on_chip = jnp.logical_and(me >= first, me < first + m)
     owning = jnp.logical_and(on_chip, core == 1)
     resting = jnp.logical_not(owning)
@@ -156,7 +167,6 @@
         ],
         axis=0,
     )
-    squares = jnp.sum(x * x, axis=-1, keepdims=True)
     g = gain[...].astype(F32)
     scaled = jnp.concatenate(
         [x[:, i * HD : (i + 1) * HD] * g[i : i + 1] for i in range(g.shape[0])], axis=1
@@ -164,19 +174,25 @@
     upper = scaled.astype(BF16)
     lower = (scaled - upper.astype(F32)).astype(BF16)
     both = jnp.concatenate([upper, lower], axis=0)
-    for j in range(m):
-        qsend[j, 0] = jnp.broadcast_to(squares[j * share : (j + 1) * share], (share, HD))
+    def place_squares():
+        squares = jnp.sum(x * x, axis=-1, keepdims=True)
+        for j in range(m):
+            qsend[j, squared] = jnp.broadcast_to(squares[j * share : (j + 1) * share], (share, HD))
+
+
+    def unit_of(head):
+        return sum(edge <= head for edge in units) - 1
 
     def span(c):
-        start = cuts[c] + 1 if c else 0
-        return pl.ds(start, cuts[c + 1] + 1 - start)
+        start = cuts[c] + (cuts[c] >= squared)
+        return pl.ds(start, cuts[c + 1] + (cuts[c + 1] >= squared) - start)
 
     def partial_send(c, j):
         return pltpu.make_async_remote_copy(
             src_ref=qsend.at[j, span(c)],
             dst_ref=qrecv.at[2 * me + core, span(c)],
             send_sem=qs_send,
-            recv_sem=qs_recv.at[cuts[c] // hc],
+            recv_sem=qs_recv.at[unit_of(cuts[c])],
             device_id=device(first + j, 1),
             device_id_type=MESH,
         )
@@ -195,9 +211,11 @@
         part = product[:rows] + product[rows:]
         for h in range(cuts[c + 1] - cuts[c]):
             for j in range(m):
-                qsend[j, cuts[c] + h + 1] = part[
+                qsend[j, cuts[c] + (cuts[c] >= squared) + h] = part[
                     j * share : (j + 1) * share, h * HD : (h + 1) * HD
                 ]
+        if cuts[c + 1] == squared:
+            place_squares()
         if c == 0:
             pl.semaphore_wait(barrier, greeted)
         for j in range(m):
@@ -208,112 +226,160 @@
     ins[4].wait()
     newf[...] = newb[...].astype(F32)
 
-    def query_sends(c):
+    def flip(k):
+        j = lax.rem(my_j + k, m)
+        for r in range(piece):
+            kturn[j * piece + r] = kbuf[j * piece + r].T
+
+    later[0].wait()
+    flip(0)
+
+    @pl.when(resting)
+    def _():
+        for k in range(1, m):
+            flip(k)
+
+    lanes = lax.broadcasted_iota(jnp.int32, (full, HD), 1)
+    lanes = lanes - lax.broadcasted_iota(jnp.int32, (full, HD), 0) * each
+
+    tiles = [
+        (units[i] // hc, pl.ds(units[i] % hc * 2, (units[i + 1] - units[i]) * 2))
+        for i in range(len(units) - 1)
+    ]
+
+    def query_sends(i):
+        c, part = tiles[i]
         return [
             (
                 not_me(z, u),
                 pltpu.make_async_remote_copy(
-                    src_ref=qall.at[c, my_j] if u else qown.at[c],
-                    dst_ref=qall.at[c, my_j],
+                    src_ref=(qall.at[c, my_j] if u else qown.at[c]).at[:, part],
+                    dst_ref=qall.at[c, my_j].at[:, part],
                     send_sem=qg_send,
-                    recv_sem=qg_recv.at[c, my_j],
+                    recv_sem=qg_recv.at[i, my_j],
                     device_id=device(z, u),
                     device_id_type=MESH,
                 ),
             )
-            for z in reversed(order)
             for u in (0, 1)
+            for z in order
         ]
 
     @pl.when(owning)
     def _():
-        for c in range(chunks):
-            lo = 0 if c == 0 else 1 + c * hc
-            arrived = qrecv.at[pl.ds(0, 2 * n - 1), pl.ds(lo, 1 + (c + 1) * hc - lo)]
-            pltpu.make_async_copy(arrived, arrived, qs_recv.at[c]).wait()
-            total = functools.reduce(jnp.add, [qrecv[2 * z + 1, 0] for z in range(n)])
+        for i in range(len(units) - 1):
+            c, part = tiles[i]
+            size = units[i + 1] - units[i]
+            lo = units[i] + (i > 0)
+            arrived = qrecv.at[pl.ds(0, 2 * n - 1), pl.ds(lo, size + (i == 0))]
+            pltpu.make_async_copy(arrived, arrived, qs_recv.at[i]).wait()
+            total = functools.reduce(jnp.add, [qrecv[2 * z + 1, squared] for z in range(n)])
             inv = lax.rsqrt(total / width + EPS) * (1.0 / HD**0.5)
-            for h in (0, 1):
-                planes = pl.ds(1 + c * hc, hc)
-                q = functools.reduce(jnp.add, [qrecv[2 * z + h, planes] for z in range(n)])
-                qturn[h * hc : (h + 1) * hc] = (q * inv[None]).astype(BF16).astype(F32)
+            for t in range(size // 4):
+                for h in (0, 1):
+                    planes = pl.ds(lo + t * 4, 4)
+                    q = functools.reduce(jnp.add, [qrecv[2 * z + h, planes] for z in range(n)])
+                    q = (q * inv[None]).astype(BF16).astype(F32)
+                    qturn[t * 8 + h * 4 : t * 8 + h * 4 + 4] = q
             for r in range(piece):
-                qown[c, r] = qturn[:, r, :]
-                qall[c, my_j, r] = qturn[:, piece + r, :]
-            for go, copy in query_sends(c):
+                qown[c, r, part] = qturn[: 2 * size, r, :]
+                qall[c, my_j, r, part] = qturn[: 2 * size, piece + r, :]
+            for go, copy in query_sends(i):
                 pl.when(go)(copy.start)
+            if units[i + 1] == hc:
+                for k in range(1, m):
+                    flip(k)
 
     lanes = lax.broadcasted_iota(jnp.int32, (full, HD), 1)
-    lanes = lanes - lax.broadcasted_iota(jnp.int32, (full, HD), 0) // 8 * piece
+    lanes = lanes - lax.broadcasted_iota(jnp.int32, (full, HD), 0) * each
     positions = me * block + lax.broadcasted_iota(jnp.int32, (full, block), 1)
 
     def keep_own(c):
-        arecv[c, 1, me] = asend[c, my_j]
-
-    def result_send(c, j):
+        for s in range(subs):
+            arecv[c, s, 1, me] = asend[c, my_j, s]
+            srecv[c, s, n + me] = ssend[c, my_j, s]
+
+    def stats_send(c, j, s):
         return pltpu.make_async_remote_copy(
-            src_ref=asend.at[c, j],
-            dst_ref=arecv.at[c, core, me],
-            send_sem=as_send,
-            recv_sem=as_recv.at[c, core],
+            src_ref=ssend.at[c, j, s],
+            dst_ref=srecv.at[c, s, core * n + me],
+            send_sem=ss_send,
+            recv_sem=ss_recv.at[c, s],
             device_id=device(first + j, 1),
             device_id_type=MESH,
         )
 
+    def result_send(c, j, s):
+        return pltpu.make_async_remote_copy(
+            src_ref=asend.at[c, j, s],
+            dst_ref=arecv.at[c, s, core, me],
+            send_sem=as_send,
+            recv_sem=as_recv.at[c, s, core],
+            device_id=device(first + j, 1),
+            device_id_type=MESH,
+        )
+
+    adds = jnp.where(me == n // 2, 1.0, 0.0)
+
     for c in range(chunks):
         for k in range(m):
-            j = lax.rem(my_j + k, m)
-            arrival = pltpu.make_async_remote_copy(
-                src_ref=qall.at[c, j],
-                dst_ref=qall.at[c, j],
-                send_sem=qg_send,
-                recv_sem=qg_recv.at[c, j],
-                device_id=device(me, other),
-                device_id_type=MESH,
-            )
-            pl.when(not_me(first + j, 1))(arrival.wait_recv)
-            if c == 0 and k == 0:
-                later[0].wait()
+            j = lax.rem(my_j + m - 1 - k, m)
+            for i, (chunk, part) in enumerate(tiles):
+                if chunk == c:
+                    arrival = pltpu.make_async_remote_copy(
+                        src_ref=qall.at[c, j].at[:, part],
+                        dst_ref=qall.at[c, j].at[:, part],
+                        send_sem=qg_send,
+                        recv_sem=qg_recv.at[i, j],
+                        device_id=device(me, other),
+                        device_id_type=MESH,
+                    )
+                    pl.when(not_me(first + j, 1))(arrival.wait_recv)
             scores, own = [], []
             for r in range(piece):
                 q = qall[c, j, r]
                 scores.append(
-                    lax.dot_general(
-                        q.astype(BF16),
-                        kbuf[j * piece + r],
-                        (((1,), (1,)), ((), ())),
-                        preferred_element_type=F32,
-                    )
+                    jnp.dot(q.astype(BF16), kturn[j * piece + r], preferred_element_type=F32)
                 )
                 row = core * half_rows + j * piece + r
                 own.append(jnp.sum(q * newf[0, pl.ds(row, 1)], axis=-1, keepdims=True))
             if c == 0 and k == 0:
                 later[1].wait()
-            stats = jnp.zeros((full, HD), F32)
-            for r in range(piece):
-                live = positions < lens_ref[core * half_rows + j * piece + r]
-                masked = jnp.where(live, scores[r], -jnp.inf)
-                top = jnp.maximum(jnp.max(masked, axis=-1, keepdims=True), own[r])
-                weights = jnp.exp(masked - top)
-                weight = jnp.sum(weights, axis=-1, keepdims=True)
-                for i, column in enumerate((top, weight, own[r])):
-                    stats = jnp.where(lanes == i * wide + r, column, stats)
-                asend[c, j, r * full : (r + 1) * full] = jnp.dot(
-                    weights.astype(BF16), vbuf[j * piece + r], preferred_element_type=F32
-                )
-            asend[c, j, piece * full : piece * full + 8] = functools.reduce(
-                jnp.add, [stats[i : i + 8] for i in range(0, full, 8)]
-            )
-            pl.when(not_me(first + j, 1))(result_send(c, j).start)
+            for s in range(subs):
+                stats = jnp.zeros((full, HD), F32)
+                for i in range(part_rows):
+                    r = s * part_rows + i
+                    row = core * half_rows + j * piece + r
+                    live = positions < lens_ref[row]
+                    masked = jnp.where(live, scores[r], -jnp.inf)
+                    top = jnp.maximum(jnp.max(masked, axis=-1, keepdims=True), own[r])
+                    weights = jnp.exp(masked - top)
+                    fresh = jnp.exp(own[r] - top) * adds
+                    weight = jnp.sum(weights, axis=-1, keepdims=True) + fresh
+                    stats = jnp.where(lanes == 2 * i, top, stats)
+                    stats = jnp.where(lanes == 2 * i + 1, weight, stats)
+                    product = jnp.dot(
+                        weights.astype(BF16), vbuf[j * piece + r], preferred_element_type=F32
+                    )
+                    product = product + fresh * newf[1, pl.ds(row, 1)]
+                    asend[c, j, s, i * full : (i + 1) * full] = product
+                ssend[c, j, s] = jnp.sum(stats, axis=0, keepdims=True)
+
+            @pl.when(not_me(first + j, 1))
+            def _(c=c, j=j):
+                for s in range(subs):
+                    stats_send(c, j, s).start()
+                    result_send(c, j, s).start()
+
             pl.when(is_me(first + j, 1))(functools.partial(keep_own, c))
 
-    def returns(c, u, stops):
-        group = pl.ds(u * half_rows + my_j * piece, piece)
+    def returns(c, s, u, stops):
+        group = pl.ds(u * half_rows + my_j * piece + s * part_rows, part_rows)
         return [
             (
                 not_me(z, h),
                 pltpu.make_async_remote_copy(
-                    src_ref=att.at[c, group] if h else aout.at[c, u],
+                    src_ref=att.at[c, group] if h else aout.at[c, s, u],
                     dst_ref=att.at[c, group],
                     send_sem=ag_send,
                     recv_sem=ag_recv.at[c],
@@ -325,44 +391,54 @@
             for h in (0, 1)
         ]
 
+    def share_out(c, s):
+        arrived = srecv.at[c, s, pl.ds(0, 2 * n - 1)]
+        pltpu.make_async_copy(arrived, arrived, ss_recv.at[c, s]).wait()
+        for u in (1, 0):
+            stats = [jnp.broadcast_to(srecv[c, s, u * n + z], (8, HD)) for z in range(n)]
+            top = functools.reduce(jnp.maximum, stats)
+            factors = [jnp.exp(line - top) for line in stats]
+            totals = functools.reduce(
+                jnp.add, [pltpu.roll(stats[z], HD - 1, 1) * factors[z] for z in range(n)]
+            )
+            inverse = 1.0 / totals
+            for i in range(part_rows):
+                for t in range(full // 8):
+                    here = lanes[t * 8 : t * 8 + 8] == 2 * i
+                    at = i * full + t * 8
+                    for z, factor in enumerate(factors):
+                        one = jnp.where(here, factor * inverse, 0.0)
+                        one = jnp.sum(one, axis=-1, keepdims=True)
+                        coef[u, z, at : at + 8] = jnp.broadcast_to(one, (8, HD))
+
     @pl.when(owning)
     def _():
         for c in range(chunks):
-            for u in (1, 0):
-                arrived = arecv.at[c, u, pl.ds(0, n - u)]
-                pltpu.make_async_copy(arrived, arrived, as_recv.at[c, u]).wait()
-                stats = [arecv[c, u, z, piece * full : piece * full + 8] for z in range(n)]
-                tops = [s[:, :wide] for s in stats]
-                top = functools.reduce(jnp.maximum, tops)
-                fresh = jnp.exp(stats[0][:, 2 * wide : 3 * wide] - top)
-                factors = [jnp.exp(t - top) for t in tops]
-                totals = fresh
-                for z in range(n):
-                    totals = totals + stats[z][:, wide : 2 * wide] * factors[z]
-                inverse = 1.0 / totals
-                fresh = fresh * inverse
-                factors = [f * inverse for f in factors]
-                for r in range(piece):
-                    row = u * half_rows + my_j * piece + r
-                    for t in range(full // 8):
-                        at = t * piece + r
-                        result = fresh[:, at : at + 1] * newf[1, pl.ds(row, 1)]
-                        for z in range(n):
-                            part = arecv[c, u, z, r * full + t * 8 : r * full + t * 8 + 8]
-                            result = result + part * factors[z][:, at : at + 1]
-                        result = result.astype(BF16).astype(F32)
-                        if t * 8 < hc:
-                            aout[c, u, r, t * 8 : t * 8 + 8] = result
-                        else:
-                            att[c, row, t * 8 - hc : t * 8 - hc + 8] = result
-                if c < chunks - 1:
-                    ready = returns(c, u, order)
-                else:
-                    ready = returns(c, u, order[:2])
-                    if u == 0:
-                        ready += returns(c, 1, order[2:]) + returns(c, 0, order[2:])
-                for go, copy in ready:
-                    pl.when(go)(copy.start)
+            for s in range(subs):
+                last = c == chunks - 1 and s == subs - 1
+                share_out(c, s)
+                for u in (1, 0):
+                    arrived = arecv.at[c, s, u, pl.ds(0, n - u)]
+                    pltpu.make_async_copy(arrived, arrived, as_recv.at[c, s, u]).wait()
+                    for i in range(part_rows):
+                        row = u * half_rows + my_j * piece + s * part_rows + i
+                        for t in range(full // 8):
+                            at = slice(i * full + t * 8, i * full + t * 8 + 8)
+                            result = functools.reduce(
+                                jnp.add,
+                                [coef[u, z, at] * arecv[c, s, u, z, at] for z in range(n)],
+                            )
+                            result = result.astype(BF16).astype(F32)
+                            aout[c, s, u, i, t * 4 : t * 4 + 4] = result[:4]
+                            att[c, row, t * 4 : t * 4 + 4] = result[4:]
+                    if not last:
+                        ready = returns(c, s, u, order)
+                    else:
+                        ready = returns(c, s, u, order[:2])
+                        if u == 0:
+                            ready += returns(c, s, 1, order[2:]) + returns(c, s, 0, order[2:])
+                    for go, copy in ready:
+                        pl.when(go)(copy.start)
 
     sent, kept = None, None
     for c in range(chunks):
@@ -399,11 +475,13 @@
     def _():
         drain(qsend, qs_send)
         drain(asend, as_send)
+        drain(ssend, ss_send)
 
     @pl.when(owning)
     def _():
         drain(qsend.at[pl.ds(0, m - 1)], qs_send)
         drain(asend.at[:, pl.ds(0, m - 1)], as_send)
+        drain(ssend.at[:, pl.ds(0, m - 1)], ss_send)
         drain(tally, qg_send)
         drain(tally, ag_send)
 
@@ -417,6 +495,8 @@
         heads = wq.shape[1] // HD
         share = rows // m
         piece = share // 2
+        subs = 1
+        units = tuple(heads * e // UNITS[-1] for e in UNITS)
         block = keys.shape[1]
         half = wout.shape[1] // 2
         hc = heads // CHUNKS
@@ -424,7 +504,7 @@
         anywhere = pl.BlockSpec(memory_space=pl.ANY)
         dma = pltpu.SemaphoreType.DMA
         return pl.pallas_call(
-            functools.partial(kernel, n, heads, rows, m, cuts, CHUNKS),
+            functools.partial(kernel, n, heads, rows, m, cuts, CHUNKS, units),
             out_shape=pltpu.VMEM((rows, half), F32),
             in_specs=[anywhere] * 9,
             out_specs=pl.BlockSpec(memory_space=pltpu.VMEM),
@@ -443,9 +523,13 @@
                 pltpu.VMEM((2 * hc, share, HD), F32),
                 pltpu.VMEM((CHUNKS, piece, 2 * hc, HD), F32),
                 pltpu.VMEM((CHUNKS, m, piece, 2 * hc, HD), F32),
-                pltpu.VMEM((CHUNKS, m, piece * 2 * hc + 8, HD), F32),
-                pltpu.VMEM((CHUNKS, 2, n, piece * 2 * hc + 8, HD), F32),
-                pltpu.VMEM((CHUNKS, 2, piece, hc, HD), F32),
+                pltpu.VMEM((rows // 2, HD, block), BF16),
+                pltpu.VMEM((CHUNKS, m, subs, 1, HD), F32),
+                pltpu.VMEM((CHUNKS, subs, 2 * n, 1, HD), F32),
+                pltpu.VMEM((2, n, piece // subs * 2 * hc, HD), F32),
+                pltpu.VMEM((CHUNKS, m, subs, piece // subs * 2 * hc, HD), F32),
+                pltpu.VMEM((CHUNKS, subs, 2, n, piece // subs * 2 * hc, HD), F32),
+                pltpu.VMEM((CHUNKS, subs, 2, piece // subs, hc, HD), F32),
                 pltpu.VMEM((CHUNKS, rows, hc, HD), F32),
                 pltpu.VMEM((rows, half), F32),
                 pltpu.VMEM((rows, half), F32),
@@ -455,11 +539,13 @@
                 dma((2,)),
                 dma(()),
                 dma(()),
-                dma((CHUNKS,)),
+                dma((len(units) - 1,)),
                 dma(()),
-                dma((CHUNKS, m)),
+                dma((len(units) - 1, m)),
                 dma(()),
-                dma((CHUNKS, 2)),
+                dma((CHUNKS, subs)),
+                dma(()),
+                dma((CHUNKS, subs, 2)),
                 dma(()),
                 dma((CHUNKS,)),
                 dma((2,)),

time: 22.4 us -> 21.8 us (0.973)
  Pallas kernels: 21.7 us -> 21 us
    pallas_call x1, Pallas kernels: 21.7 us -> 21 us  [shards(): pl.pallas_call(functools.partial(kernel, n, heads, rows, m, cuts, CHUNKS,...]
where the time goes in v4:
time: 21.8 us; the launch traced here: 21.6 us
  Pallas kernels  21 us (96%)
  local copies, waits for them, and re-layouts  0.62 us (3%)
    pallas_call x1, Pallas kernels, shards(): pl.pallas_call(functools.partial(kernel, n, heads, rows, m, cuts, CHUNKS,...  21 us
    unnamed x1, local copies, waits for them, and re-layouts  0.62 us

profile of v4, /device:TPU:0, one launch (start us, length us, event | category | flops | bytes accessed | tf_op | source)
XLA Modules:
  0.0 21.6 jit_solution(6835099639320791785)
XLA Ops:
  0.0 21.0 %decode_step.1 = f32[16,512]{1,0:T(8,128)S(1)} custom-call(s32[16]{0:T(128)} %lens_hbm.1, bf16[16,1024]{1,0:T(8,128)(2,1)} %hidden_hbm.1, bf16[8,128]{1,0:T(8,128)(2,1)} %bitcast.1, bf16[1024,2048]{1,0:T(8,128)(2,1)} %wq_hbm.1, bf16[16,1024,128]{2,1,0:T(8,128)(2,1)} %keys_hbm.1, bf16[16,1024,128]{2,1,0:T(8,128)(2,1)} %values_hbm.1, ...), custom_call_target="tpu_custom_call" | custom-call | tf_op jit(solution)/shard_map/decode_step/pallas_call | solution.py:506
  21.0 0.6 %copy.11 = f32[16,512]{1,0:T(8,128)} copy(f32[16,512]{1,0:T(8,128)S(1)} %decode_step.1) | data formatting | bytes 65536

commit v5 on v4

--- a/solution.py
+++ b/solution.py
@@ -14,7 +14,7 @@
 BF16 = jnp.bfloat16
 EDGES = (0, 2, 4, 8, 16)
 CHUNKS = 2
-UNITS = (0, 4, 8, 16)
+UNITS = (0, 2, 4, 8, 16)
 
 
 def outside_in(n):
@@ -247,6 +247,23 @@
         for i in range(len(units) - 1)
     ]
 
+    def runs_of(c):
+        heads_at = []
+        for lo, hi in zip(units[:-1], units[1:]):
+            if lo // hc == c:
+                heads_at += [(h, head % hc) for h in (0, 1) for head in range(lo, hi)]
+        found = []
+        for t in range(full // 8):
+            found.append([])
+            for at, (h, head) in enumerate(heads_at[t * 8 : t * 8 + 8]):
+                if at and found[t][-1][1] == h and found[t][-1][2] + found[t][-1][3] == head:
+                    found[t][-1][3] += 1
+                else:
+                    found[t].append([at, h, head, 1])
+        return found
+
+    runs = [runs_of(c) for c in range(chunks)]
+
     def query_sends(i):
         c, part = tiles[i]
         return [
@@ -275,12 +292,11 @@
             pltpu.make_async_copy(arrived, arrived, qs_recv.at[i]).wait()
             total = functools.reduce(jnp.add, [qrecv[2 * z + 1, squared] for z in range(n)])
             inv = lax.rsqrt(total / width + EPS) * (1.0 / HD**0.5)
-            for t in range(size // 4):
-                for h in (0, 1):
-                    planes = pl.ds(lo + t * 4, 4)
-                    q = functools.reduce(jnp.add, [qrecv[2 * z + h, planes] for z in range(n)])
-                    q = (q * inv[None]).astype(BF16).astype(F32)
-                    qturn[t * 8 + h * 4 : t * 8 + h * 4 + 4] = q
+            for h in (0, 1):
+                planes = pl.ds(lo, size)
+                q = functools.reduce(jnp.add, [qrecv[2 * z + h, planes] for z in range(n)])
+                q = (q * inv[None]).astype(BF16).astype(F32)
+                qturn[h * size : (h + 1) * size] = q
             for r in range(piece):
                 qown[c, r, part] = qturn[: 2 * size, r, :]
                 qall[c, my_j, r, part] = qturn[: 2 * size, piece + r, :]
@@ -429,8 +445,12 @@
                                 [coef[u, z, at] * arecv[c, s, u, z, at] for z in range(n)],
                             )
                             result = result.astype(BF16).astype(F32)
-                            aout[c, s, u, i, t * 4 : t * 4 + 4] = result[:4]
-                            att[c, row, t * 4 : t * 4 + 4] = result[4:]
+                            for at, h, head, size in runs[c][t]:
+                                span_in = slice(at, at + size)
+                                if h:
+                                    att[c, row, head : head + size] = result[span_in]
+                                else:
+                                    aout[c, s, u, i, head : head + size] = result[span_in]
                     if not last:
                         ready = returns(c, s, u, order)
                     else:

time: 21.8 us -> 21.6 us (level)
  no operation moved by 1% of the time
where the time goes in v5:
time: 21.6 us; the launch traced here: 21.5 us
  Pallas kernels  20.8 us (96%)
  local copies, waits for them, and re-layouts  0.62 us (3%)
    pallas_call x1, Pallas kernels, shards(): pl.pallas_call(functools.partial(kernel, n, heads, rows, m, cuts, CHUNKS,...  20.8 us
    unnamed x1, local copies, waits for them, and re-layouts  0.62 us

profile of v5, /device:TPU:0, one launch (start us, length us, event | category | flops | bytes accessed | tf_op | source)
XLA Modules:
  0.0 21.5 jit_solution(17189434034584279990)
XLA Ops:
  0.0 20.8 %decode_step.1 = f32[16,512]{1,0:T(8,128)S(1)} custom-call(s32[16]{0:T(128)} %lens_hbm.1, bf16[16,1024]{1,0:T(8,128)(2,1)} %hidden_hbm.1, bf16[8,128]{1,0:T(8,128)(2,1)} %bitcast.1, bf16[1024,2048]{1,0:T(8,128)(2,1)} %wq_hbm.1, bf16[16,1024,128]{2,1,0:T(8,128)(2,1)} %keys_hbm.1, bf16[16,1024,128]{2,1,0:T(8,128)(2,1)} %values_hbm.1, ...), custom_call_target="tpu_custom_call" | custom-call | tf_op jit(solution)/shard_map/decode_step/pallas_call | solution.py:526
  20.8 0.6 %copy.11 = f32[16,512]{1,0:T(8,128)} copy(f32[16,512]{1,0:T(8,128)S(1)} %decode_step.1) | data formatting | bytes 65536
